TPU v7x, 32 devices: a whole 2x2x4 slice. The times are simulated.
32 devices in a mesh: dp: 32 (over z, y, x, core).
Axes of the slice: x: 2, y: 2, z: 4, core: 2. Of those that a mesh axis runs over, the one named last changes fastest.
Arguments:
- hidden: bfloat16 [24576, 2560], P('dp'), may hold values from -16 to 16
- rotation: bfloat16 [2560, 2560], P('dp'), may hold values from -1 to 1, as said below
- norm_gain: float32 [2, 2560], replicated, may hold values from 0.1 to 1.9
- value_weight: bfloat16 [2, 2560, 1024], P(None, None, 'dp'), may hold values from -0.125 to 0.125
- output_weight: bfloat16 [2, 1024, 2560], P(None, 'dp'), may hold values from -0.1875 to 0.1875
- lengths: int32 [32], replicated, may hold values from 1 to 768, as said below
Outputs:
- rotated_out: bfloat16 [24576, 2560], P('dp')
- calib_loss: float32 [], replicated
Inputs may be any that keep to these rules, and one draw needn't show every extreme that they name: `lengths`: some device has all of its 768 rows live. `rotation`: an orthogonal matrix rounded to bfloat16.
All inputs are finite; a program needn't handle non-finite values.
Results may differ from a plain program's by a relative error of at most 0.0088.
Values may be sent and summed in bfloat16 or wider, within the bound.
A program may use at most 192 MiB of HBM per device.

v0:
```python
import jax
import jax.numpy as jnp
from jax import lax
from jax.sharding import PartitionSpec as P

BLOCK = 256
SLOTS = 3


EPS_NORM = 1e-06
EPS_SCALE = 1e-06
CLIP_RATIO = 0.9
TWO_PI = 6.283185307179586


def soft_round(values):
    return values - jnp.sin(TWO_PI * values) / TWO_PI


def fake_quant(values, step_size):
    return soft_round(jnp.clip(values / step_size, -8.0, 7.0)) * step_size


def quantize_with(matrix, column_tops):
    return fake_quant(matrix, column_tops / 7.0 + EPS_SCALE).astype(jnp.bfloat16)


def rotate_weights(rotation_full, norm_gain, value_weight, output_weight):
    layer_count = norm_gain.shape[0]
    value_cols = value_weight.shape[2]
    output_rows = output_weight.shape[1]
    pieces = []
    for number in range(layer_count):
        scaled = (norm_gain[number][:, None] * value_weight[number].astype(jnp.float32)).astype(
            jnp.bfloat16
        )
        pieces.append(scaled)
        pieces.append(jnp.transpose(output_weight[number]))
    joined = jnp.concatenate(pieces, axis=1)
    product = lax.dot_general(
        rotation_full, joined, (((0,), (0,)), ((), ())), preferred_element_type=jnp.float32
    )
    value_list = []
    output_list = []
    offset = 0
    for number in range(layer_count):
        rotated_v = product[:, offset : offset + value_cols]
        value_list.append(quantize_with(rotated_v, jnp.max(jnp.abs(rotated_v), axis=0)[None, :]))
        offset = offset + value_cols
        output_list.append(jnp.transpose(product[:, offset : offset + output_rows]))
        offset = offset + output_rows
    return (value_list, output_list)


def per_device(hidden, rotation, norm_gain, value_weight, output_weight, lengths):
    own_index = lax.axis_index("dp")
    width = hidden.shape[1]
    layer_count = norm_gain.shape[0]
    rotation_full = lax.all_gather(rotation, "dp", axis=0, tiled=True)
    value_list, output_list = rotate_weights(rotation_full, norm_gain, value_weight, output_weight)
    value_local = jnp.stack(value_list)
    output_local = jnp.stack(output_list)
    output_tops = lax.pmax(jnp.max(jnp.abs(output_local), axis=1), "dp")
    value_all = lax.all_gather(value_local, "dp", axis=2, tiled=True)
    output_all = lax.all_gather(
        quantize_with(output_local, output_tops[:, None, :]), "dp", axis=1, tiled=True
    )
    own_len = lax.dynamic_index_in_dim(lengths, own_index, 0, keepdims=False)
    own_blocks = (own_len + BLOCK - 1) // BLOCK
    x_blocks = hidden.reshape(SLOTS, BLOCK, width)
    slot_range = jnp.arange(SLOTS, dtype=jnp.int32)
    own_valid = jnp.clip(own_len - slot_range * BLOCK, 0, BLOCK)
    done_slots = slot_range < own_blocks
    work_slots = x_blocks.shape[0]
    active = (jnp.arange(BLOCK, dtype=jnp.int32)[None, :] < own_valid[:, None]) & done_slots[
        :, None
    ]

    def slot_of(step_number):
        return jnp.where(step_number < own_blocks, step_number, SLOTS + step_number - own_blocks)

    def rotate_step(step_number, resid_buf):
        slot_pos = slot_of(step_number)
        block_rows = lax.dynamic_index_in_dim(x_blocks, slot_pos, 0, keepdims=False)
        rotated = jnp.dot(block_rows, rotation_full, preferred_element_type=jnp.float32)
        return lax.dynamic_update_index_in_dim(resid_buf, rotated, slot_pos, 0)

    resid_buf = lax.fori_loop(
        0, own_blocks, rotate_step, jnp.zeros((work_slots, BLOCK, width), jnp.float32)
    )
    local_loss = jnp.zeros((), jnp.float32)
    for layer_number in range(layer_count):
        value_q = value_all[layer_number]
        output_q = output_all[layer_number]
        channels = value_q.shape[1]

        def first_step(step_number, carry):
            square_buf, error_buf, mixed_buf, channel_top = carry
            slot_pos = slot_of(step_number)
            residual = lax.dynamic_index_in_dim(resid_buf, slot_pos, 0, keepdims=False)
            live_mask = lax.dynamic_index_in_dim(active, slot_pos, 0, keepdims=False)
            mean_sq = jnp.mean(residual * residual, axis=1)
            normed = residual * lax.rsqrt(mean_sq + EPS_NORM)[:, None]
            step_size = CLIP_RATIO * jnp.max(jnp.abs(normed), axis=1) / 7.0 + EPS_SCALE
            act_f = fake_quant(normed, step_size[:, None])
            act_err = jnp.sum((act_f - normed) * (act_f - normed), axis=1)
            mixed = jnp.dot(act_f.astype(jnp.bfloat16), value_q, preferred_element_type=jnp.float32)
            channel_top = jnp.maximum(
                channel_top, jnp.max(jnp.where(live_mask[:, None], jnp.abs(mixed), 0.0), axis=0)
            )
            square_buf = lax.dynamic_update_index_in_dim(square_buf, mean_sq, slot_pos, 0)
            error_buf = lax.dynamic_update_index_in_dim(error_buf, act_err, slot_pos, 0)
            mixed_buf = lax.dynamic_update_index_in_dim(mixed_buf, mixed, slot_pos, 0)
            return (square_buf, error_buf, mixed_buf, channel_top)

        first_init = (
            jnp.zeros((work_slots, BLOCK), jnp.float32),
            jnp.zeros((work_slots, BLOCK), jnp.float32),
            jnp.zeros((work_slots, BLOCK, channels), jnp.float32),
            jnp.zeros((channels,), jnp.float32),
        )
        square_buf, error_buf, mixed_buf, channel_top = lax.fori_loop(
            0, own_blocks, first_step, first_init
        )
        vrange = lax.pmax(channel_top, "dp")
        mix_step = CLIP_RATIO * vrange / 7.0 + EPS_SCALE

        def second_step(step_number, carry):
            residual_all, mix_error_buf = carry
            slot_pos = slot_of(step_number)
            residual = lax.dynamic_index_in_dim(residual_all, slot_pos, 0, keepdims=False)
            mixed = lax.dynamic_index_in_dim(mixed_buf, slot_pos, 0, keepdims=False)
            mix_f = fake_quant(mixed, mix_step[None, :])
            mix_err = jnp.sum((mix_f - mixed) * (mix_f - mixed), axis=1)
            updated = residual + jnp.dot(
                mix_f.astype(jnp.bfloat16), output_q, preferred_element_type=jnp.float32
            )
            residual_all = lax.dynamic_update_index_in_dim(residual_all, updated, slot_pos, 0)
            mix_error_buf = lax.dynamic_update_index_in_dim(mix_error_buf, mix_err, slot_pos, 0)
            return (residual_all, mix_error_buf)

        resid_buf, mix_error_buf = lax.fori_loop(
            0, own_blocks, second_step, (resid_buf, jnp.zeros((work_slots, BLOCK), jnp.float32))
        )
        local_loss = local_loss + jnp.sum(
            jnp.where(active, square_buf * (error_buf + mix_error_buf), 0.0)
        )
    out_work = jnp.where(active[:, :, None], resid_buf, 0.0).astype(jnp.bfloat16)
    loss_sum = lax.psum(local_loss, "dp")
    count = jnp.sum(lengths).astype(jnp.float32)
    return (out_work.reshape(SLOTS * BLOCK, width), loss_sum / count)


def solution(mesh):
    return jax.shard_map(
        per_device,
        mesh=mesh,
        in_specs=(P("dp", None), P("dp", None), P(), P(None, None, "dp"), P(None, "dp", None), P()),
        out_specs=(P("dp", None), P()),
        check_vma=False,
    )
```

profile of v0, /device:TPU:0, one launch (start us, length us, event | category | flops | bytes accessed | tf_op | source)
XLA Modules:
  0.0 703.4 jit_solution(10541958787850556832)
XLA Ops:
  7.2 0.0 all-gather.4.cloned.1.call-start
  7.2 0.7 all-gather.4.cloned.1.call-update
  7.9 0.0 all-gather.6.cloned.1.call-start
  7.9 0.9 slice_reduce_fusion.1
  8.8 1.0 slice_bitcast_fusion.7
  9.8 1.1 fusion.30
  10.9 100.4 %all-gather.4.cloned.1.call-done = bf16[2560,2560]{1,0:T(8,128)(2,1)} async-done(((bf16[80,2560]{1,0:T(8,128)(2,1)}), bf16[2560,2560]{1,0:T(8,128)(2,1)}) %all-gather.4.cloned.1.call-update) | async-done | bytes 13107216 | tf_op jit(solution)/shard_map/all_gather | solution.py:59
  111.3 6.6 convolution_bitcast_fusion.1
  117.9 0.0 copy-start.9
  117.9 0.2 abs_reduce_fusion.4
  118.1 2.4 slice_bitcast_fusion.5
  120.5 0.0 copy-start.4
  120.5 0.8 pad_maximum_fusion.1
  121.3 0.0 all-gather.6.cloned.1.call-update
  121.3 0.0 all-gather.8.cloned.1.call-start
  121.4 0.0 copy-done.9
  121.4 0.6 dynamic_slice.47
  122.7 0.7 subtract_clamp_fusion
  123.3 0.0 copy-start.5
  123.3 0.1 fusion.33
  123.4 0.1 abs_reduce_fusion.2
  123.5 4.1 broadcast_in_dim.118
  127.6 0.0 copy-done.5
  127.6 10.4 %while.70 = (s32[]{:T(128)}, f32[3,256,2560]{2,1,0:T(8,128)}, s32[]{:T(128)}, bf16[3,256,2560]{2,1,0:T(8,128)(2,1)}, bf16[2560,2560]{1,0:T(8,128)(2,1)}, /*index=5*/s32[]{:T(128)}, s32[]{:T(128)}, s32[]{:T(128)}) while((s32[]{:T(128)}, f32[3,256,2560]{2,1,0:T(8,128)}, s32[]{:T(128)}, bf16[3,256,2560]{2,1,0:T(8,128)(2,1)}, ...), condition=%wide.region_1.2_spmd, body=%wide.region_0.0_spmd.sunk | while | flops 3355443200 | bytes 17040548 | solution.py:88
  127.6 10.4 %fusion.58 = f32[3,256,2560]{2,1,0:T(8,128)} fusion(f32[3,256,2560]{2,1,0:T(8,128)} %get-tuple-element.738, s32[]{:T(128)S(6)} %select_n.121, bf16[2560,2560]{1,0:T(8,128)(2,1)} %get-tuple-element.749, bf16[3,256,2560]{2,1,0:T(8,128)(2,1)} %get-tuple-element.748), kind=kOutput, calls=%fused_computation.1.clone.1 | convolution fusion | flops 3355443200 | bytes 17040384 | tf_op jit(solution)/shard_map/while/body/dot_general | solution.py:85
  138.0 68.1 %all-gather.6.cloned.1.call-done = bf16[2,2560,1024]{1,2,0:T(8,128)(2,1)} async-done(((bf16[2,2560,32]{1,2,0:T(8,128)(2,1)}), bf16[2,2560,1024]{1,2,0:T(8,128)(2,1)}) %all-gather.6.cloned.1.call-update) | async-done | bytes 10485776 | tf_op jit(solution)/shard_map/all_gather | solution.py:64
  206.1 8.7 %slice_bitcast_fusion.1 = (bf16[2560,1024]{0,1:T(8,128)(2,1)}, bf16[2560,1024]{0,1:T(8,128)(2,1)}) fusion(bf16[2,2560,1024]{1,2,0:T(8,128)(2,1)} %all-gather.6.cloned.1.call-done), kind=kLoop, calls=%fused_computation.57 | loop fusion | bytes 20971520 | tf_op jit(solution)/shard_map/squeeze | solution.py:93
  214.7 8.0 %copy.8 = bf16[2560,1024]{1,0:T(8,128)(2,1)} copy(bf16[2560,1024]{0,1:T(8,128)(2,1)} %get-tuple-element.470) | data formatting | bytes 10485760 | tf_op jit(solution)/shard_map/while | solution.py:122
  222.7 0.4 broadcast.252.clone
  223.1 27.8 %while.71 = (s32[]{:T(128)}, f32[3,256]{1,0:T(4,128)S(1)}, f32[3,256]{1,0:T(4,128)S(1)}, f32[3,256,1024]{2,1,0:T(8,128)S(1)}, f32[1024]{0:T(1024)S(1)}, /*index=...) while((s32[]{:T(128)}, f32[3,256]{1,0:T(4,128)S(1)}, ...), condition=%wide.region_9.10_spmd, body=%wide.region_4.9_spmd.sunk | while | flops 1358037248 | bytes 39881720 | solution.py:122
  223.3 2.1 fusion.60
  225.5 2.3 abs_reduce_fusion.7
  227.8 11.8 %bitcast_dynamic-update-slice_fusion.4 = (f32[3,256,1024]{2,1,0:T(8,128)S(1)}, f32[256,1024]{1,0:T(8,128)S(1)}) fusion(f32[3,256,1024]{2,1,0:T(8,128)S(1)} %get-tuple-element.768, s32[]{:T(128)S(6)} %select_n.124, bf16[2560,1024]{1,0:T(8,128)(2,1)S(1)} %copy-done.3, f32[256]{0:T(256)S(1)} %multiply_add_fusion.9, f32[256]{0:T(256)S(1)} %get-tuple-element.699, ...), kind=kOutput, calls=%fused_computation.35.clone.1 | convolution fusion | flops 1347420160 | bytes 9964544 | tf_op jit(solution)/shard_map/while/body/dot_general | solution.py:107
  239.7 0.2 select_reduce_fusion.6
  239.9 10.9 %multiply_reduce_fusion.4 = f32[256]{0:T(256)S(1)} fusion(f32[3,256,2560]{2,1,0:T(8,128)} %get-tuple-element.783, s32[]{:T(128)S(6)} %select_n.124, f32[256]{0:T(256)S(1)} %get-tuple-element.699, f32[256]{0:T(256)S(1)} %multiply_add_fusion.9), kind=kLoop, calls=%fused_computation.30.clone.1 | loop fusion | flops 6553344 | bytes 2624516 | tf_op jit(solution)/shard_map/while/body/reduce_sum | solution.py:106
  250.9 94.2 %all-reduce = (f32[1024]{0:T(1024)S(1)}, f32[2,2560]{1,0:T(2,128)S(1)}) all-reduce(f32[1024]{0:T(1024)S(1)} %get-tuple-element.348, f32[2,2560]{1,0:T(2,128)S(1)} %abs_reduce_fusion.2), channel_id=1, replica_groups=mesh['dp'=32] {'dp'}, use_global_device_ids=true, to_apply=%region_10.11 | all-reduce | flops 6144 | bytes 49152 | tf_op jit(solution)/shard_map/pmax | solution.py:125
  345.1 3.9 multiply_convert_fusion
  348.9 0.0 all-gather.8.cloned.1.call-update
  349.0 0.7 reduce_sum.95
  349.7 8.0 %copy.9 = bf16[2560,1024]{1,0:T(8,128)(2,1)} copy(bf16[2560,1024]{0,1:T(8,128)(2,1)} %get-tuple-element.469) | data formatting | bytes 10485760 | tf_op jit(solution)/shard_map/while | solution.py:122
  357.6 78.1 %all-gather.8.cloned.1.call-done = bf16[2,1024,2560]{2,1,0:T(8,128)(2,1)} async-done(((bf16[2,32,2560]{2,1,0:T(8,128)(2,1)}), bf16[2,1024,2560]{2,1,0:T(8,128)(2,1)}) %all-gather.8.cloned.1.call-update) | async-done | bytes 10485776 | tf_op jit(solution)/shard_map/all_gather | solution.py:65
  435.8 8.6 %slice_bitcast_fusion = (bf16[1024,2560]{1,0:T(8,128)(2,1)}, bf16[1024,2560]{1,0:T(8,128)(2,1)}) fusion(bf16[2,1024,2560]{2,1,0:T(8,128)(2,1)} %all-gather.8.cloned.1.call-done), kind=kLoop, calls=%fused_computation.56 | loop fusion | bytes 20971520 | tf_op jit(solution)/shard_map/squeeze | solution.py:94
  444.4 13.8 %while.72 = (s32[]{:T(128)}, f32[3,256,2560]{2,1,0:T(8,128)}, f32[3,256]{1,0:T(4,128)S(1)}, s32[]{:T(128)}, f32[3,256,1024]{2,1,0:T(8,128)S(1)}, /*index=5*/f32[...) while((s32[]{:T(128)}, f32[3,256,2560]{2,1,0:T(8,128)}, ...), condition=%wide.region_15.16_spmd, body=%wide.region_13.15_spmd.sunk | while | flops 1347026688 | bytes 38809820 | solution.py:142
  444.6 2.1 constant_dynamic-slice_fusion.4
  446.7 1.2 copy-done.1
  447.9 6.2 fusion.63
  454.1 4.0 fusion.64
  458.2 0.4 broadcast.252
  458.6 27.6 %while.73 = (s32[]{:T(128)}, f32[3,256]{1,0:T(4,128)S(1)}, f32[3,256]{1,0:T(4,128)S(1)}, f32[3,256,1024]{2,1,0:T(8,128)S(1)}, f32[1024]{0:T(1024)S(1)}, /*index=...) while((s32[]{:T(128)}, f32[3,256]{1,0:T(4,128)S(1)}, ...), condition=%wide.region_21.22_spmd, body=%wide.region_16.21_spmd.sunk | while | flops 1358037248 | bytes 39881720 | solution.py:122
  458.6 0.0 copy-start.2
  458.6 2.1 fusion.66
  460.8 2.3 abs_reduce_fusion.8
  463.1 11.8 %bitcast_dynamic-update-slice_fusion.5 = (f32[3,256,1024]{2,1,0:T(8,128)S(1)}, f32[256,1024]{1,0:T(8,128)S(1)}) fusion(f32[3,256,1024]{2,1,0:T(8,128)S(1)} %get-tuple-element.834, s32[]{:T(128)S(6)} %select_n.129, bf16[2560,1024]{1,0:T(8,128)(2,1)S(1)} %copy-done.2, f32[256]{0:T(256)S(1)} %multiply_add_fusion.10, f32[256]{0:T(256)S(1)} %get-tuple-element.719, ...), kind=kOutput, calls=%fused_computation.49.clone.1 | convolution fusion | flops 1347420160 | bytes 9964544 | tf_op jit(solution)/shard_map/while/body/dot_general | solution.py:107
  475.0 0.2 select_reduce_fusion.7
  475.2 10.9 %multiply_reduce_fusion.5 = f32[256]{0:T(256)S(1)} fusion(f32[3,256,2560]{2,1,0:T(8,128)} %get-tuple-element.849, s32[]{:T(128)S(6)} %select_n.129, f32[256]{0:T(256)S(1)} %get-tuple-element.719, f32[256]{0:T(256)S(1)} %multiply_add_fusion.10), kind=kLoop, calls=%fused_computation.44.clone.1 | loop fusion | flops 6553344 | bytes 2624516 | tf_op jit(solution)/shard_map/while/body/reduce_sum | solution.py:106
  486.2 121.2 %pmax.23 = f32[1024]{0:T(1024)S(1)} all-reduce(f32[1024]{0:T(1024)S(1)} %get-tuple-element.351), channel_id=1, replica_groups=mesh['dp'=32] {'dp'}, use_global_device_ids=true, to_apply=%region_22.23 | all-reduce | flops 1024 | bytes 8192 | tf_op jit(solution)/shard_map/pmax | solution.py:125
  607.4 13.8 %while.74 = (s32[]{:T(128)}, f32[3,256,2560]{2,1,0:T(8,128)}, f32[3,256]{1,0:T(4,128)S(1)}, s32[]{:T(128)}, f32[3,256,1024]{2,1,0:T(8,128)S(1)}, /*index=5*/f32[...) while((s32[]{:T(128)}, f32[3,256,2560]{2,1,0:T(8,128)}, ...), condition=%wide.region_25.26_spmd, body=%wide.region_23.25_spmd.sunk | while | flops 1347026688 | bytes 38809820 | solution.py:142
  607.7 2.1 constant_dynamic-slice_fusion.5
  609.7 1.2 copy-done
  610.9 6.2 fusion.69
  617.1 4.0 fusion.70
  621.2 0.7 select_reduce_fusion.2
  623.9 65.1 %psum.7 = f32[]{:T(128)} all-reduce(f32[]{:T(128)S(6)} %add.189), channel_id=1, replica_groups=mesh['dp'=32] {'dp'}, use_global_device_ids=true, to_apply=%region_28.29 | all-reduce | flops 1 | bytes 8 | tf_op jit(solution)/shard_map/psum | solution.py:149
  688.9 5.7 select_convert_fusion
  (39 shorter events, 0.4 us)
Async XLA Ops:
  7.2 104.1 %all-gather.4.cloned.1.call-start = ((), (), s32[]{:S(2)}) async-start(), calls=%async_computation | async-start | bytes 13516800 | tf_op jit(solution)/shard_map/all_gather | solution.py:59
  7.9 198.2 %all-gather.6.cloned.1.call-start = ((), (), s32[]{:S(2)}) async-start(), calls=%async_computation.1 | async-start | bytes 10813440 | tf_op jit(solution)/shard_map/all_gather | solution.py:64
  117.9 3.5 copy-start.9
  120.5 7.1 %copy-start.4 = (f32[1,32,2560]{2,1,0:T(8,128)}, f32[1,32,2560]{2,1,0:T(8,128)S(1)}, u32[]{:S(2)}) copy-start(f32[1,32,2560]{2,1,0:T(8,128)S(1)} %get-tuple-element.473) | copy-start | bytes 983044
  121.3 314.4 %all-gather.8.cloned.1.call-start = ((), (), s32[]{:S(2)}) async-start(), calls=%async_computation.2 | async-start | bytes 10813440 | tf_op jit(solution)/shard_map/all_gather | solution.py:65
  123.3 4.3 copy-start.5
  123.3 4.2 copy-start.7
  223.3 4.5 copy-start.3
  444.6 3.3 copy-start.1
  458.6 4.5 copy-start.2
  607.3 13.9 %copy-start.6 = (s32[3]{0:T(128)S(1)}, s32[3]{0:T(128)}, u32[]{:S(2)}) copy-start(s32[3]{0:T(128)} %copy-done.5) | copy-start | bytes 40
  607.4 13.9 %copy-start.8 = (pred[3]{0:T(512)(128)(4,1)S(1)}, pred[3]{0:T(512)(128)(4,1)}, u32[]{:S(2)}) copy-start(pred[3]{0:T(512)(128)(4,1)} %copy-done.7) | copy-start | bytes 13
  607.6 3.3 copy-start
Sparse Core Ops, SparseCore 0:
  10.8 100.4 all-gather.3
  121.5 84.5 all-gather.5
  349.1 86.6 all-gather.7
where the time goes:
time: 710 us; the launch traced here: 703 us
  blocking collectives  280 us (39%)
  waiting for transfers between devices  247 us (35%)
  other arithmetic  55.4 us (8%)
  matrix products  53 us (7%)
  local copies, waits for them, and re-layouts  47.4 us (7%)
  between operations  18.8 us (3%)
    pmax x2, blocking collectives, per_device(): vrange = lax.pmax(channel_top, 'dp')  215 us
    all_gather x1, waiting for transfers between devices, per_device(): rotation_full = lax.all_gather(rotation, 'dp', axis=0, tiled=True)  100 us
    all_gather x1, waiting for transfers between devices, per_device(): lax.all_gather(quantize_with(output_local, output_tops[:, None, :]), 'dp'...  78.1 us
    all_gather x1, waiting for transfers between devices, per_device(): value_all = lax.all_gather(value_local, 'dp', axis=2, tiled=True)  68.1 us
    psum x1, blocking collectives, per_device(): loss_sum = lax.psum(local_loss, 'dp')  65.1 us
    dot_general x2, matrix products, first_step(): jnp.dot(act_f.astype(jnp.bfloat16), value_q, preferred_element_type=jnp.f...  23.7 us
    reduce_sum x2, other arithmetic, first_step(): act_err = jnp.sum((act_f - normed) * (act_f - normed), axis=1)  21.8 us
    while x2, local copies, waits for them, and re-layouts, per_device(): lax.fori_loop(0, own_blocks, first_step, first_init)  15.9 us
  transfers between devices with their start and end apart: 3, of which 3 were waited for; matrix products, arithmetic and copies ran while one was open for 4% of the time, Pallas kernels for 0%

commit v1 on v0

v1 whole, which is shorter than its diff:
```python
import functools

import jax
import jax.numpy as jnp
from jax import lax
from jax.experimental import pallas as pl
from jax.experimental.pallas import tpu as pltpu
from jax.sharding import PartitionSpec as P

BLOCK = 256
CHUNK = 16
TILE = 512
VMEM_LIMIT = 60 * 1024 * 1024

EPS_NORM = 1e-06
EPS_SCALE = 1e-06
CLIP_RATIO = 0.9
POLY = (0.9999997571452157, -2.579687436847881, 2.6673586060553345, -1.5145036626283546, 0.48039577352173)


def soft_round(values):
    r = values - jnp.round(values)
    u = r * r
    p = jnp.float32(POLY[-1])
    for c in POLY[-2::-1]:
        p = p * u + jnp.float32(c)
    return values - p * (r - 4.0 * (r * u))


def fake_quant(values, step_size):
    inv = 1.0 / step_size
    return soft_round(jnp.clip(values * inv, -8.0, 7.0)) * step_size


def weight_kernel(v_rows, o_rows, layers, w_ref, r_ref, vq_ref, o_ref, top_ref, acc):
    j = pl.program_id(0)
    n = r_ref.shape[1]
    at = pl.ds(pl.multiple_of(j * n, n), n)
    prod = jnp.dot(w_ref[...], r_ref[...], preferred_element_type=jnp.float32)
    acc[:, at] = prod[:v_rows]
    o_ref[...] = prod[v_rows:]
    per = o_rows // layers
    for l in range(layers):
        lo = v_rows + l * per
        top_ref[l : l + 1, :] = jnp.max(jnp.abs(prod[lo : lo + per]), axis=0, keepdims=True)

    @pl.when(j == pl.num_programs(0) - 1)
    def _():
        def body(i, _):
            rows = pl.ds(pl.multiple_of(i * CHUNK, CHUNK), CHUNK)
            x = acc[rows, :]
            step = jnp.max(jnp.abs(x), axis=1, keepdims=True) / 7.0 + EPS_SCALE
            vq_ref[rows, :] = fake_quant(x, step).astype(jnp.bfloat16)
            return 0

        lax.fori_loop(0, v_rows // CHUNK, body, 0)


def rotate_weights(joined, rotation, v_rows, o_rows, layers):
    width = rotation.shape[1]
    depth = rotation.shape[0]
    return pl.pallas_call(
        functools.partial(weight_kernel, v_rows, o_rows, layers),
        name="rotate_weights",
        grid=(width // TILE,),
        in_specs=[
            pl.BlockSpec(joined.shape, lambda j: (0, 0)),
            pl.BlockSpec((depth, TILE), lambda j: (0, j)),
        ],
        out_specs=[
            pl.BlockSpec((v_rows, width), lambda j: (0, 0)),
            pl.BlockSpec((o_rows, TILE), lambda j: (0, j)),
            pl.BlockSpec((layers, TILE), lambda j: (0, j)),
        ],
        out_shape=[
            jax.ShapeDtypeStruct((v_rows, width), jnp.bfloat16),
            jax.ShapeDtypeStruct((o_rows, width), jnp.float32),
            jax.ShapeDtypeStruct((layers, width), jnp.float32),
        ],
        scratch_shapes=[pltpu.VMEM((v_rows, width), jnp.float32)],
        compiler_params=pltpu.CompilerParams(vmem_limit_bytes=VMEM_LIMIT),
        cost_estimate=pl.CostEstimate(
            flops=2 * joined.shape[0] * depth * width,
            bytes_accessed=2 * depth * width,
            transcendentals=0,
        ),
    )(joined, rotation)


def norm_rows(resid_ref, act_ref, msq_ref, aerr_ref):
    width = resid_ref.shape[1]

    def body(i, _):
        rows = pl.ds(pl.multiple_of(i * CHUNK, CHUNK), CHUNK)
        x = resid_ref[rows, :]
        mean_sq = jnp.sum(x * x, axis=1, keepdims=True) * (1.0 / width)
        inv = lax.rsqrt(mean_sq + EPS_NORM)
        step = CLIP_RATIO * (jnp.max(jnp.abs(x), axis=1, keepdims=True) * inv) / 7.0 + EPS_SCALE
        normed = x * inv
        act = fake_quant(normed, step)
        diff = act - normed
        act_ref[rows, :] = act.astype(jnp.bfloat16)
        msq_ref[rows, :] = mean_sq
        aerr_ref[rows, :] = jnp.sum(diff * diff, axis=1, keepdims=True)
        return 0

    lax.fori_loop(0, resid_ref.shape[0] // CHUNK, body, 0)


def first_kernel(h_ref, r_ref, resid_ref, act_ref, msq_ref, aerr_ref):
    def body(j, _):
        at = pl.ds(pl.multiple_of(j * TILE, TILE), TILE)
        resid_ref[:, at] = jnp.dot(h_ref[...], r_ref[:, at], preferred_element_type=jnp.float32)
        return 0

    lax.fori_loop(0, r_ref.shape[1] // TILE, body, 0)
    norm_rows(resid_ref, act_ref, msq_ref, aerr_ref)


def rows_spec(width):
    return pl.BlockSpec((BLOCK, width), lambda i, *_: (i, 0))


def whole_spec(shape):
    return pl.BlockSpec(shape, lambda i, *_: (0, 0), pipeline_mode=pl.Buffered(1))


def act_shapes(rows, width):
    return [
        jax.ShapeDtypeStruct((rows, width), jnp.float32),
        jax.ShapeDtypeStruct((rows, width), jnp.bfloat16),
        jax.ShapeDtypeStruct((rows, 1), jnp.float32),
        jax.ShapeDtypeStruct((rows, 1), jnp.float32),
    ]


def first_pass(hidden, rotation):
    rows, depth = hidden.shape
    width = rotation.shape[1]
    return pl.pallas_call(
        first_kernel,
        name="rotate_hidden",
        grid=(rows // BLOCK,),
        in_specs=[rows_spec(depth), whole_spec(rotation.shape)],
        out_specs=[rows_spec(width), rows_spec(width), rows_spec(1), rows_spec(1)],
        out_shape=act_shapes(rows, width),
        compiler_params=pltpu.CompilerParams(vmem_limit_bytes=VMEM_LIMIT),
        cost_estimate=pl.CostEstimate(
            flops=2 * rows * depth * width,
            bytes_accessed=2 * depth * width + 8 * rows * width,
            transcendentals=0,
        ),
    )(hidden, rotation)


def mix_kernel(len_ref, act_ref, v_ref, mixed_ref, top_ref):
    i = pl.program_id(0)
    tile = 256
    live = len_ref[0] - i * BLOCK
    mask = lax.broadcasted_iota(jnp.int32, (BLOCK, 1), 0) < live

    @pl.when(i == 0)
    def _():
        top_ref[...] = jnp.zeros_like(top_ref)

    def body(j, _):
        at = pl.ds(pl.multiple_of(j * tile, tile), tile)
        prod = lax.dot_general(
            act_ref[...],
            v_ref[at, :],
            (((1,), (1,)), ((), ())),
            preferred_element_type=jnp.float32,
        )
        mixed_ref[:, at] = prod
        peak = jnp.max(jnp.where(mask, jnp.abs(prod), 0.0), axis=0, keepdims=True)
        top_ref[:, at] = jnp.maximum(top_ref[:, at], peak)
        return 0

    lax.fori_loop(0, v_ref.shape[0] // tile, body, 0)


def mix_pass(own_len, act, values):
    rows, width = act.shape
    channels = values.shape[0]
    return pl.pallas_call(
        mix_kernel,
        name="mix",
        grid_spec=pltpu.PrefetchScalarGridSpec(
            num_scalar_prefetch=1,
            grid=(rows // BLOCK,),
            in_specs=[rows_spec(width), whole_spec(values.shape)],
            out_specs=[
                rows_spec(channels),
                pl.BlockSpec((1, channels), lambda i, *_: (0, 0)),
            ],
        ),
        out_shape=[
            jax.ShapeDtypeStruct((rows, channels), jnp.float32),
            jax.ShapeDtypeStruct((1, channels), jnp.float32),
        ],
        compiler_params=pltpu.CompilerParams(vmem_limit_bytes=VMEM_LIMIT),
        cost_estimate=pl.CostEstimate(
            flops=2 * rows * channels * width,
            bytes_accessed=2 * channels * width + 4 * rows * width,
            transcendentals=0,
        ),
    )(own_len, act, values)


def update_kernel(last, len_ref, mixed_ref, vrange_ref, o_ref, resid_ref, msq_ref, aerr_ref, *rest):
    if last:
        loss_ref, out_ref, mix_buf = rest
    else:
        loss_ref, new_ref, act_ref, nmsq_ref, naerr_ref, mix_buf = rest
    live = len_ref[0] - pl.program_id(0) * BLOCK
    mask = lax.broadcasted_iota(jnp.int32, (BLOCK, 1), 0) < live
    step = CLIP_RATIO * vrange_ref[...] / 7.0 + EPS_SCALE

    def quant(i, _):
        rows = pl.ds(pl.multiple_of(i * CHUNK, CHUNK), CHUNK)
        x = mixed_ref[rows, :]
        mix = fake_quant(x, step)
        diff = mix - x
        mix_buf[rows, :] = mix.astype(jnp.bfloat16)
        loss_ref[rows, :] = jnp.sum(diff * diff, axis=1, keepdims=True)
        return 0

    lax.fori_loop(0, BLOCK // CHUNK, quant, 0)
    loss_ref[...] = jnp.where(mask, msq_ref[...] * (aerr_ref[...] + loss_ref[...]), 0.0)

    def body(j, _):
        at = pl.ds(pl.multiple_of(j * TILE, TILE), TILE)
        new = resid_ref[:, at] + jnp.dot(
            mix_buf[...], o_ref[:, at], preferred_element_type=jnp.float32
        )
        if last:
            out_ref[:, at] = jnp.where(mask, new, 0.0).astype(jnp.bfloat16)
        else:
            new_ref[:, at] = new
        return 0

    lax.fori_loop(0, o_ref.shape[1] // TILE, body, 0)
    if not last:
        norm_rows(new_ref, act_ref, nmsq_ref, naerr_ref)


def update_pass(own_len, mixed, vrange, outputs, resid, msq, aerr, last):
    rows, width = resid.shape
    channels = mixed.shape[1]
    out_specs = [rows_spec(1)]
    out_shape = [jax.ShapeDtypeStruct((rows, 1), jnp.float32)]
    if last:
        out_specs.append(rows_spec(width))
        out_shape.append(jax.ShapeDtypeStruct((rows, width), jnp.bfloat16))
    else:
        out_specs += [rows_spec(width), rows_spec(width), rows_spec(1), rows_spec(1)]
        out_shape += act_shapes(rows, width)
    return pl.pallas_call(
        functools.partial(update_kernel, last),
        name="update",
        grid_spec=pltpu.PrefetchScalarGridSpec(
            num_scalar_prefetch=1,
            grid=(rows // BLOCK,),
            in_specs=[
                rows_spec(channels),
                whole_spec((1, channels)),
                whole_spec(outputs.shape),
                rows_spec(width),
                rows_spec(1),
                rows_spec(1),
            ],
            out_specs=out_specs,
            scratch_shapes=[pltpu.VMEM((BLOCK, channels), jnp.bfloat16)],
        ),
        out_shape=out_shape,
        compiler_params=pltpu.CompilerParams(vmem_limit_bytes=VMEM_LIMIT),
        cost_estimate=pl.CostEstimate(
            flops=2 * rows * channels * width,
            bytes_accessed=2 * channels * width + 12 * rows * width,
            transcendentals=0,
        ),
    )(own_len, mixed, vrange, outputs, resid, msq, aerr)


def per_device(hidden, rotation, norm_gain, value_weight, output_weight, lengths):
    layers = norm_gain.shape[0]
    cols = value_weight.shape[2]
    own_len = lax.dynamic_slice_in_dim(lengths, lax.axis_index("dp"), 1)
    scaled = (norm_gain[:, :, None] * value_weight.astype(jnp.float32)).astype(jnp.bfloat16)
    width = rotation.shape[1]
    depth = value_weight.shape[1]
    joined = jnp.concatenate(
        [
            jnp.swapaxes(scaled, 1, 2).reshape(layers * cols, depth),
            output_weight.reshape(layers * cols, depth),
        ],
        axis=0,
    )
    rotation_full = lax.all_gather(rotation, "dp", axis=0, tiled=True)
    value_q, rotated_o, tops = rotate_weights(
        joined, rotation_full, layers * cols, layers * cols, layers
    )
    tops = lax.pmax(tops, "dp")
    output_q = [
        fake_quant(
            rotated_o[l * cols : (l + 1) * cols], tops[l : l + 1] / 7.0 + EPS_SCALE
        ).astype(jnp.bfloat16)
        for l in range(layers)
    ]
    value_all = []
    output_all = []
    for l in range(layers):
        local_v = value_q[l * cols : (l + 1) * cols]
        if l > 0:
            local_v, _ = lax.optimization_barrier((local_v, output_q[l - 1]))
        value_all.append(lax.all_gather(local_v, "dp", axis=0, tiled=True))
        output_all.append(lax.all_gather(output_q[l], "dp", axis=0, tiled=True))
    hidden, _ = lax.optimization_barrier((hidden, output_q[0]))
    resid, act, msq, aerr = first_pass(hidden, rotation_full)
    loss = jnp.zeros((), jnp.float32)
    for l in range(layers):
        mixed, top = mix_pass(own_len, act, value_all[l])
        vrange = lax.pmax(top, "dp")
        last = l == layers - 1
        res = update_pass(own_len, mixed, vrange, output_all[l], resid, msq, aerr, last)
        loss = loss + jnp.sum(res[0])
        if last:
            out = res[1]
        else:
            resid, act, msq, aerr = res[1:]
    count = jnp.sum(lengths).astype(jnp.float32)
    return (out, lax.psum(loss, "dp") / count)


def solution(mesh):
    return jax.shard_map(
        per_device,
        mesh=mesh,
        in_specs=(P("dp", None), P("dp", None), P(), P(None, None, "dp"), P(None, "dp", None), P()),
        out_specs=(P("dp", None), P()),
        check_vma=False,
    )
```

time: 710 us -> 460 us (0.65)
  Pallas kernels: 0 us -> 125 us
  blocking collectives: 280 us -> 161 us
  waiting for transfers between devices: 247 us -> 145 us
  matrix products: 53 us -> 0 us
  other arithmetic: 55.4 us -> 8.42 us
  local copies, waits for them, and re-layouts: 47.4 us -> 2.33 us
    pallas_call x0 -> x6, Pallas kernels: none -> 125 us  [the longest x2 56.7 us: update_pass(): pl.pallas_call(functools.partial(update_kernel, last), name='update', gri...]
    all_gather x2 -> x4, waiting for transfers between devices: 146 us -> 43.2 us  [the longest x2 27.8 us: per_device(): value_all.append(lax.all_gather(local_v, 'dp', axis=0, tiled=True))]
    pmax x2 -> x3, blocking collectives: 215 us -> 121 us  [the longest x2 81.8 us: per_device(): vrange = lax.pmax(top, 'dp')]
    dot_general x6 -> x0, matrix products: 53 us -> none  [the longest x2 23.7 us: first_step(): jnp.dot(act_f.astype(jnp.bfloat16), value_q, preferred_element_type=jnp.f...]
    reduce_sum x7 -> x2, other arithmetic: 34.9 us -> 2.48 us  [per_device(): loss = loss + jnp.sum(res[0])]
    psum x1, blocking collectives: 65.1 us -> 39.4 us  [per_device(): return (out, lax.psum(loss, 'dp') / count)]
    while x10 -> x0, local copies, waits for them, and re-layouts: 18.3 us -> none  [the longest x2 15.9 us: per_device(): lax.fori_loop(0, own_blocks, first_step, first_init)]
    squeeze x2 -> x0, local copies, waits for them, and re-layouts: 17.3 us -> none  [the longest x1 8.68 us: per_device(): value_q = value_all[layer_number]]
  transfers between devices with their start and end apart: 3 -> 5, of which waited for: 3 -> 3; matrix products, arithmetic and copies ran while one was open for 4% -> 1% of each run, Pallas kernels for 0% -> 21%
where the time goes in v1:
time: 460 us; the launch traced here: 459 us
  blocking collectives  161 us (35%)
  waiting for transfers between devices  145 us (32%)
  Pallas kernels  125 us (27%)
  between operations  17.5 us (4%)
  other arithmetic  8.42 us (2%)
    all_gather x1, waiting for transfers between devices, per_device(): rotation_full = lax.all_gather(rotation, 'dp', axis=0, tiled=True)  100 us
    pmax x2, blocking collectives, per_device(): vrange = lax.pmax(top, 'dp')  81.8 us
    pallas_call x2, Pallas kernels, update_pass(): pl.pallas_call(functools.partial(update_kernel, last), name='update', gri...  56.7 us
    pmax x1, blocking collectives, per_device(): tops = lax.pmax(tops, 'dp')  39.5 us
    psum x1, blocking collectives, per_device(): return (out, lax.psum(loss, 'dp') / count)  39.4 us
    pallas_call x1, Pallas kernels, first_pass(): pl.pallas_call(first_kernel, name='rotate_hidden', grid=(rows // BLOCK,),...  35.9 us
    all_gather x2, waiting for transfers between devices, per_device(): value_all.append(lax.all_gather(local_v, 'dp', axis=0, tiled=True))  27.8 us
    pallas_call x2, Pallas kernels, mix_pass(): pl.pallas_call(mix_kernel, name='mix', grid_spec=pltpu.PrefetchScalarGrid...  22.6 us
  transfers between devices with their start and end apart: 5, of which 3 were waited for; matrix products, arithmetic and copies ran while one was open for 1% of the time, Pallas kernels for 21%

profile of v1, /device:TPU:0, one launch (start us, length us, event | category | flops | bytes accessed | tf_op | source)
XLA Modules:
  0.0 459.3 jit_solution(5151196718747544287)
XLA Ops:
  7.2 0.0 all-gather.6.cloned.1.call-start
  7.2 0.7 all-gather.6.cloned.1.call-update
  7.9 0.0 all-gather.8.cloned.1.call-start
  7.9 1.0 multiply_convert_fusion
  9.0 1.9 pad_maximum_fusion.w_ref
  10.8 0.0 copy-start.1
  10.8 100.4 %all-gather.6.cloned.1.call-done.r_ref = bf16[2560,2560]{1,0:T(8,128)(2,1)} async-done(((bf16[80,2560]{1,0:T(8,128)(2,1)}), bf16[2560,2560]{1,0:T(8,128)(2,1)}) %all-gather.6.cloned.1.call-update) | async-done | bytes 13107216 | tf_op jit(solution)/shard_map/all_gather | solution.py:299
  111.3 9.6 %rotate_weights.1 = (bf16[64,2560]{1,0:T(8,128)(2,1)}, f32[64,2560]{1,0:T(8,128)}, f32[2,2560]{1,0:T(2,128)}) custom-call(bf16[128,2560]{1,0:T(8,128)(2,1)} %pad_maximum_fusion.w_ref, bf16[2560,2560]{1,0:T(8,128)(2,1)} %all-gather.6.cloned.1.call-done.r_ref), custom_call_target="tpu_custom_call" | custom-call | flops 1677721600 | bytes 13107200 | tf_op jit(solution)/shard_map/rotate_weights/pallas_call | solution.py:62
  120.9 1.7 fusion.24
  122.6 0.0 all-gather.8.cloned.1.call-update
  122.6 0.0 all-gather.10.cloned.1.call-start
  122.7 39.5 %pmax.21 = f32[2,2560]{1,0:T(2,128)S(1)} all-reduce(f32[2,2560]{1,0:T(2,128)} %get-tuple-element.23), channel_id=1, replica_groups=mesh['dp'=32] {'dp'}, use_global_device_ids=true, to_apply=%region_0.0 | all-reduce | flops 5120 | bytes 40960 | tf_op jit(solution)/shard_map/pmax | solution.py:303
  162.2 0.1 divide_reduce_fusion
  162.3 2.2 fusion.18
  164.5 0.0 all-gather.10.cloned.1.call-update
  164.6 0.0 all-gather.12.cloned.1.call-start
  164.6 0.5 all-gather.12.cloned.1.call-update
  165.1 0.0 all-gather.14.cloned.1.call-start
  165.2 0.5 all-gather.14.cloned.1.call-update
  165.7 0.0 copy-done.1
  165.7 0.7 reduce_sum.29
  166.4 0.6 dynamic_slice.3.len_ref
  167.0 35.9 %rotate_hidden.1 = (f32[768,2560]{1,0:T(8,128)}, bf16[768,2560]{1,0:T(8,128)(2,1)}, f32[768,1]{1,0:T(8,128)}, f32[768,1]{1,0:T(8,128)}) custom-call(bf16[768,2560]{1,0:T(8,128)(2,1)} %h_ref, bf16[2560,2560]{1,0:T(8,128)(2,1)} %all-gather.6.cloned.1.call-done.r_ref), custom_call_target="tpu_custom_call" | custom-call | flops 10066329600 | bytes 28835840 | tf_op jit(solution)/shard_map/rotate_hidden/pallas_call | solution.py:140
  202.9 0.0 all-gather.8.cloned.1.call-done.v_ref
  202.9 11.3 %mix.2 = (f32[768,1024]{1,0:T(8,128)}, f32[1,1024]{1,0:T(1,128)}) custom-call(s32[1]{0:T(128)} %dynamic_slice.3.len_ref, bf16[768,2560]{1,0:T(8,128)(2,1)} %get-tuple-element.25.act_ref, bf16[1024,2560]{1,0:T(8,128)(2,1)} %all-gather.8.cloned.1.call-done.v_ref), custom_call_target="tpu_custom_call" | custom-call | flops 4026531840 | bytes 13107200 | tf_op jit(solution)/shard_map/mix/pallas_call | solution.py:185
  214.2 41.8 %pmax.22.vrange_ref = f32[1,1024]{1,0:T(1,128)} all-reduce(f32[1,1024]{1,0:T(1,128)} %get-tuple-element.28), channel_id=1, replica_groups=mesh['dp'=32] {'dp'}, use_global_device_ids=true, to_apply=%region_1.2 | all-reduce | flops 1024 | bytes 8192 | tf_op jit(solution)/shard_map/pmax | solution.py:323
  256.0 0.0 all-gather.10.cloned.1.call-done.o_ref
  256.0 36.8 %update.2 = (f32[768,1]{1,0:T(8,128)}, f32[768,2560]{1,0:T(8,128)}, bf16[768,2560]{1,0:T(8,128)(2,1)}, f32[768,1]{1,0:T(8,128)}, f32[768,1]{1,0:T(8,128)}) custom-call(s32[1]{0:T(128)} %dynamic_slice.3.len_ref, f32[768,1024]{1,0:T(8,128)} %get-tuple-element.27.mixed_ref, f32[1,1024]{1,0:T(1,128)} %pmax.22.vrange_ref, ...), custom_call_target="tpu_custom_call" | custom-call | flops 4026531840 | bytes 28835840 | tf_op jit(solution)/shard_map/update/pallas_call | solution.py:258
  292.9 27.8 %all-gather.12.cloned.1.call-done.v_ref = bf16[1024,2560]{1,0:T(8,128)(2,1)} async-done(((bf16[32,2560]{1,0:T(8,128)(2,1)}), bf16[1024,2560]{1,0:T(8,128)(2,1)}) %all-gather.12.cloned.1.call-update) | async-done | bytes 5242896 | tf_op jit(solution)/shard_map/all_gather | solution.py:316
  320.7 11.3 %mix.3 = (f32[768,1024]{1,0:T(8,128)}, f32[1,1024]{1,0:T(1,128)}) custom-call(s32[1]{0:T(128)} %dynamic_slice.3.len_ref, bf16[768,2560]{1,0:T(8,128)(2,1)} %get-tuple-element.32.act_ref, bf16[1024,2560]{1,0:T(8,128)(2,1)} %all-gather.12.cloned.1.call-done.v_ref), custom_call_target="tpu_custom_call" | custom-call | flops 4026531840 | bytes 13107200 | tf_op jit(solution)/shard_map/mix/pallas_call | solution.py:185
  331.9 40.0 %pmax.23.vrange_ref = f32[1,1024]{1,0:T(1,128)} all-reduce(f32[1,1024]{1,0:T(1,128)} %get-tuple-element.35), channel_id=1, replica_groups=mesh['dp'=32] {'dp'}, use_global_device_ids=true, to_apply=%region_2.3 | all-reduce | flops 1024 | bytes 8192 | tf_op jit(solution)/shard_map/pmax | solution.py:323
  371.9 15.4 %all-gather.14.cloned.1.call-done.o_ref = bf16[1024,2560]{1,0:T(8,128)(2,1)} async-done(((bf16[32,2560]{1,0:T(8,128)(2,1)}), bf16[1024,2560]{1,0:T(8,128)(2,1)}) %all-gather.14.cloned.1.call-update) | async-done | bytes 5242896 | tf_op jit(solution)/shard_map/all_gather | solution.py:317
  387.3 0.0 copy-start
  387.4 19.8 %update.3 = (f32[768,1]{1,0:T(8,128)}, bf16[768,2560]{1,0:T(8,128)(2,1)}) custom-call(s32[1]{0:T(128)} %dynamic_slice.3.len_ref, f32[768,1024]{1,0:T(8,128)} %get-tuple-element.34.mixed_ref, f32[1,1024]{1,0:T(1,128)} %pmax.23.vrange_ref, bf16[1024,2560]{1,0:T(8,128)(2,1)} %all-gather.14.cloned.1.call-done.o_ref, f32[768,2560]{1,0:T(8,128)} %get-tuple-element.36.resid_ref, ...), custom_call_target="tpu_custom_call" | custom-call | flops 4026531840 | bytes 28835840 | tf_op jit(solution)/shard_map/update/pallas_call | solution.py:258
  407.2 1.8 reduce_sum.28
  409.0 0.0 copy-done
  409.0 0.7 reduce_sum.27
  411.6 39.4 %psum.7 = f32[]{:T(128)} all-reduce(f32[]{:T(128)S(6)} %add.49), channel_id=1, replica_groups=mesh['dp'=32] {'dp'}, use_global_device_ids=true, to_apply=%region_5.6 | all-reduce | flops 1 | bytes 8 | tf_op jit(solution)/shard_map/psum | solution.py:332
Async XLA Ops:
  7.2 104.1 %all-gather.6.cloned.1.call-start = ((), (), s32[]{:S(2)}) async-start(), calls=%async_computation | async-start | bytes 13516800 | tf_op jit(solution)/shard_map/all_gather | solution.py:299
  7.9 195.0 %all-gather.8.cloned.1.call-start = ((), (), s32[]{:S(2)}) async-start(), calls=%async_computation.1 | async-start | bytes 5406720 | tf_op jit(solution)/shard_map/all_gather | solution.py:316
  10.8 154.9 %copy-start.1 = (s32[32]{0:T(128)S(1)}, s32[32]{0:T(128)}, u32[]{:S(2)}) copy-start(s32[32]{0:T(128)} %param.11) | copy-start | bytes 388
  122.6 133.4 %all-gather.10.cloned.1.call-start = ((), (), s32[]{:S(2)}) async-start(), calls=%async_computation.2 | async-start | bytes 5406720 | tf_op jit(solution)/shard_map/all_gather | solution.py:317
  164.6 156.1 %all-gather.12.cloned.1.call-start = ((), (), s32[]{:S(2)}) async-start(), calls=%async_computation.3 | async-start | bytes 5406720 | tf_op jit(solution)/shard_map/all_gather | solution.py:316
  165.1 222.2 %all-gather.14.cloned.1.call-start = ((), (), s32[]{:S(2)}) async-start(), calls=%async_computation.4 | async-start | bytes 5406720 | tf_op jit(solution)/shard_map/all_gather | solution.py:317
  387.3 21.6 %copy-start = (f32[768,1]{1,0:T(8,128)S(1)}, f32[768,1]{1,0:T(8,128)}, u32[]{:S(2)}) copy-start(f32[768,1]{1,0:T(8,128)} %get-tuple-element.40) | copy-start | bytes 9220
Sparse Core Ops, SparseCore 0:
  10.8 100.4 all-gather.5
  122.8 64.0 all-gather.7
  189.7 64.0 all-gather.9
  256.5 64.0 all-gather.11
  323.4 63.9 all-gather.13

commit v2 on v1

--- a/solution.py
+++ b/solution.py
@@ -30,6 +30,73 @@
 def fake_quant(values, step_size):
     inv = 1.0 / step_size
     return soft_round(jnp.clip(values * inv, -8.0, 7.0)) * step_size
+
+
+def exchange_kernel(n, total, x_ref, out_ref, slots, send_sem, recv_sem):
+    me = lax.axis_index("dp")
+    barrier = pltpu.get_barrier_semaphore()
+
+    def greet(k, _):
+        pl.semaphore_signal(
+            barrier,
+            inc=1,
+            device_id=(lax.rem(me + k, n),),
+            device_id_type=pl.DeviceIdType.MESH,
+        )
+        return 0
+
+    lax.fori_loop(1, n, greet, 0)
+    pl.semaphore_wait(barrier, n - 1)
+
+    def copy_to(peer, slot):
+        return pltpu.make_async_remote_copy(
+            src_ref=x_ref,
+            dst_ref=slots.at[slot],
+            send_sem=send_sem.at[peer],
+            recv_sem=recv_sem.at[slot],
+            device_id=(peer,),
+            device_id_type=pl.DeviceIdType.MESH,
+        )
+
+    def push(k, _):
+        copy_to(lax.rem(me + k, n), me).start()
+        return 0
+
+    lax.fori_loop(1, n, push, 0)
+    slots[me] = x_ref[...]
+
+    def settle(k, _):
+        peer = lax.rem(me + k, n)
+        copy = copy_to(peer, peer)
+        copy.wait_send()
+        copy.wait_recv()
+        return 0
+
+    lax.fori_loop(1, n, settle, 0)
+
+    def fold(k, acc):
+        return acc + slots[k] if total else jnp.maximum(acc, slots[k])
+
+    out_ref[...] = lax.fori_loop(1, n, fold, slots[0])
+
+
+def exchange(x, n, collective_id, total=False):
+    return pl.pallas_call(
+        functools.partial(exchange_kernel, n, total),
+        name="exchange",
+        in_specs=[pl.BlockSpec(memory_space=pltpu.VMEM)],
+        out_specs=pl.BlockSpec(memory_space=pltpu.VMEM),
+        out_shape=jax.ShapeDtypeStruct(x.shape, x.dtype),
+        scratch_shapes=[
+            pltpu.VMEM((n,) + x.shape, x.dtype),
+            pltpu.SemaphoreType.DMA((n,)),
+            pltpu.SemaphoreType.DMA((n,)),
+        ],
+        compiler_params=pltpu.CompilerParams(
+            collective_id=collective_id, has_side_effects=True, vmem_limit_bytes=VMEM_LIMIT
+        ),
+        cost_estimate=pl.CostEstimate(flops=0, bytes_accessed=30_000_000, transcendentals=0),
+    )(x)
 
 
 def weight_kernel(v_rows, o_rows, layers, w_ref, r_ref, vq_ref, o_ref, top_ref, acc):
@@ -163,11 +230,15 @@
     def _():
         top_ref[...] = jnp.zeros_like(top_ref)
 
+    cols = v_ref.shape[1]
+    group = tile // cols
+
     def body(j, _):
         at = pl.ds(pl.multiple_of(j * tile, tile), tile)
+        part = v_ref[pl.ds(j * group, group)]
         prod = lax.dot_general(
             act_ref[...],
-            v_ref[at, :],
+            part.reshape(tile, part.shape[2]),
             (((1,), (1,)), ((), ())),
             preferred_element_type=jnp.float32,
         )
@@ -176,19 +247,28 @@
         top_ref[:, at] = jnp.maximum(top_ref[:, at], peak)
         return 0
 
-    lax.fori_loop(0, v_ref.shape[0] // tile, body, 0)
-
-
-def mix_pass(own_len, act, values):
+    lax.fori_loop(0, v_ref.shape[0] // group, body, 0)
+
+
+def mix_pass(own_len, act, gathered, layer, cols):
     rows, width = act.shape
-    channels = values.shape[0]
+    n = gathered.shape[0]
+    channels = n * cols
+    if cols % 16 == 0:
+        values = gathered
+        spec = pl.BlockSpec(
+            (n, cols, width), lambda i, *_: (0, layer, 0), pipeline_mode=pl.Buffered(1)
+        )
+    else:
+        values = gathered[:, layer * cols : (layer + 1) * cols].reshape(-1, 128, width)
+        spec = pl.BlockSpec(values.shape, lambda i, *_: (0, 0, 0), pipeline_mode=pl.Buffered(1))
     return pl.pallas_call(
         mix_kernel,
         name="mix",
         grid_spec=pltpu.PrefetchScalarGridSpec(
             num_scalar_prefetch=1,
             grid=(rows // BLOCK,),
-            in_specs=[rows_spec(width), whole_spec(values.shape)],
+            in_specs=[rows_spec(width), spec],
             out_specs=[
                 rows_spec(channels),
                 pl.BlockSpec((1, channels), lambda i, *_: (0, 0)),
@@ -300,27 +380,25 @@
     value_q, rotated_o, tops = rotate_weights(
         joined, rotation_full, layers * cols, layers * cols, layers
     )
-    tops = lax.pmax(tops, "dp")
+    n = lax.axis_size("dp")
+    tops = exchange(tops, n, 0)
     output_q = [
         fake_quant(
             rotated_o[l * cols : (l + 1) * cols], tops[l : l + 1] / 7.0 + EPS_SCALE
         ).astype(jnp.bfloat16)
         for l in range(layers)
     ]
-    value_all = []
+    value_all = lax.all_gather(value_q, "dp", axis=0, tiled=False)
     output_all = []
     for l in range(layers):
-        local_v = value_q[l * cols : (l + 1) * cols]
-        if l > 0:
-            local_v, _ = lax.optimization_barrier((local_v, output_q[l - 1]))
-        value_all.append(lax.all_gather(local_v, "dp", axis=0, tiled=True))
-        output_all.append(lax.all_gather(output_q[l], "dp", axis=0, tiled=True))
-    hidden, _ = lax.optimization_barrier((hidden, output_q[0]))
+        before = output_all[l - 1] if l > 0 else value_all
+        local_o, _ = lax.optimization_barrier((output_q[l], before))
+        output_all.append(lax.all_gather(local_o, "dp", axis=0, tiled=True))
     resid, act, msq, aerr = first_pass(hidden, rotation_full)
     loss = jnp.zeros((), jnp.float32)
     for l in range(layers):
-        mixed, top = mix_pass(own_len, act, value_all[l])
-        vrange = lax.pmax(top, "dp")
+        mixed, top = mix_pass(own_len, act, value_all, l, cols)
+        vrange = exchange(top, n, 1)
         last = l == layers - 1
         res = update_pass(own_len, mixed, vrange, output_all[l], resid, msq, aerr, last)
         loss = loss + jnp.sum(res[0])
@@ -329,7 +407,8 @@
         else:
             resid, act, msq, aerr = res[1:]
     count = jnp.sum(lengths).astype(jnp.float32)
-    return (out, lax.psum(loss, "dp") / count)
+    loss = exchange(jnp.full((1, 128), loss, jnp.float32), n, 2, total=True)[0, 0]
+    return (out, loss / count)
 
 
 def solution(mesh):

time: 460 us -> 442 us (0.961)
  blocking collectives: 161 us -> 0 us
  waiting for transfers between devices: 145 us -> 235 us
  Pallas kernels: 125 us -> 178 us
    pmax x3 -> x0, blocking collectives: 121 us -> none  [the longest x2 81.8 us: per_device(): vrange = lax.pmax(top, 'dp')]
    all_gather x4 -> x3, waiting for transfers between devices: 43.2 us -> 134 us  [the longest x2 67.2 us: per_device(): output_all.append(lax.all_gather(local_o, 'dp', axis=0, tiled=True))]
    pallas_call x0 -> x4, Pallas kernels: none -> 53.2 us  [exchange(): pl.pallas_call(functools.partial(exchange_kernel, n, total), name='exchan...]
    psum x1 -> x0, blocking collectives: 39.4 us -> none  [per_device(): return (out, lax.psum(loss, 'dp') / count)]
  transfers between devices with their start and end apart: 5 -> 4, of which waited for: 3 -> 3; matrix products, arithmetic and copies ran while one was open for 1% -> 2% of each run, Pallas kernels for 21% -> 31%
where the time goes in v2:
time: 442 us; the launch traced here: 441 us
  waiting for transfers between devices  235 us (53%)
  Pallas kernels  178 us (40%)
  between operations  17.5 us (4%)
  other arithmetic  9.07 us (2%)
    all_gather x1, waiting for transfers between devices, per_device(): rotation_full = lax.all_gather(rotation, 'dp', axis=0, tiled=True)  100 us
    all_gather x2, waiting for transfers between devices, per_device(): output_all.append(lax.all_gather(local_o, 'dp', axis=0, tiled=True))  67.2 us
    all_gather x1, waiting for transfers between devices, per_device(): value_all = lax.all_gather(value_q, 'dp', axis=0, tiled=False)  66.7 us
    pallas_call x2, Pallas kernels, update_pass(): pl.pallas_call(functools.partial(update_kernel, last), name='update', gri...  56.7 us
    pallas_call x4, Pallas kernels, exchange(): pl.pallas_call(functools.partial(exchange_kernel, n, total), name='exchan...  53.2 us
    pallas_call x1, Pallas kernels, first_pass(): pl.pallas_call(first_kernel, name='rotate_hidden', grid=(rows // BLOCK,),...  35.8 us
    pallas_call x2, Pallas kernels, mix_pass(): pl.pallas_call(mix_kernel, name='mix', grid_spec=pltpu.PrefetchScalarGrid...  22.7 us
    pallas_call x1, Pallas kernels, rotate_weights(): pl.pallas_call(functools.partial(weight_kernel, v_rows, o_rows, layers),...  9.61 us
  transfers between devices with their start and end apart: 4, of which 3 were waited for; matrix products, arithmetic and copies ran while one was open for 2% of the time, Pallas kernels for 31%

profile of v2, /device:TPU:0, one launch (start us, length us, event | category | flops | bytes accessed | tf_op | source)
XLA Modules:
  0.0 441.1 jit_solution(14004499083140990641)
XLA Ops:
  7.2 0.0 all-gather.6.cloned.1.call-start
  7.2 0.7 all-gather.6.cloned.1.call-update
  7.9 0.0 all-gather.12.cloned.1.call-start
  7.9 1.0 multiply_convert_fusion
  9.0 1.9 pad_maximum_fusion.w_ref
  10.8 0.0 copy-start.1
  10.8 100.4 %all-gather.6.cloned.1.call-done.r_ref = bf16[2560,2560]{1,0:T(8,128)(2,1)} async-done(((bf16[80,2560]{1,0:T(8,128)(2,1)}), bf16[2560,2560]{1,0:T(8,128)(2,1)}) %all-gather.6.cloned.1.call-update) | async-done | bytes 13107216 | tf_op jit(solution)/shard_map/all_gather | solution.py:379
  111.3 9.6 %rotate_weights.1 = (bf16[64,2560]{1,0:T(8,128)(2,1)}, f32[64,2560]{1,0:T(8,128)}, f32[2,2560]{1,0:T(2,128)}) custom-call(bf16[128,2560]{1,0:T(8,128)(2,1)} %pad_maximum_fusion.w_ref, bf16[2560,2560]{1,0:T(8,128)(2,1)} %all-gather.6.cloned.1.call-done.r_ref), custom_call_target="tpu_custom_call" | custom-call | flops 1677721600 | bytes 13107200 | tf_op jit(solution)/shard_map/rotate_weights/pallas_call | solution.py:129
  120.9 0.0 all-gather.12.cloned.1.call-update
  120.9 0.0 all-gather.8.cloned.1.call-start
  121.0 21.1 %exchange.5 = f32[2,2560]{1,0:T(2,128)} custom-call(f32[2,2560]{1,0:T(2,128)} %get-tuple-element.27.x_ref), custom_call_target="tpu_custom_call" | custom-call | bytes 30000000 | tf_op jit(solution)/shard_map/exchange/pallas_call | solution.py:84
  142.1 0.9 divide_reduce_fusion
  143.0 2.2 fusion.18
  145.3 66.7 %all-gather.12.cloned.1.call-done = bf16[2048,2560]{1,0:T(8,128)(2,1)} async-done(((bf16[64,2560]{1,0:T(8,128)(2,1)}), bf16[2048,2560]{1,0:T(8,128)(2,1)}) %all-gather.12.cloned.1.call-update) | async-done | bytes 10485776 | tf_op jit(solution)/shard_map/all_gather | solution.py:391
  211.9 0.0 all-gather.8.cloned.1.call-update
  211.9 0.0 all-gather.10.cloned.1.call-start
  212.0 67.2 %all-gather.8.cloned.1.call-done.o_ref = bf16[1024,2560]{1,0:T(8,128)(2,1)} async-done(((bf16[32,2560]{1,0:T(8,128)(2,1)}), bf16[1024,2560]{1,0:T(8,128)(2,1)}) %all-gather.8.cloned.1.call-update) | async-done | bytes 5242896 | tf_op jit(solution)/shard_map/all_gather | solution.py:396
  279.2 0.0 all-gather.10.cloned.1.call-update
  279.3 0.0 copy-done.1
  279.3 0.6 reduce_sum.29
  279.9 0.6 dynamic_slice.3.len_ref
  281.1 35.8 %rotate_hidden.1 = (f32[768,2560]{1,0:T(8,128)}, bf16[768,2560]{1,0:T(8,128)(2,1)}, f32[768,1]{1,0:T(8,128)}, f32[768,1]{1,0:T(8,128)}) custom-call(bf16[768,2560]{1,0:T(8,128)(2,1)} %h_ref.1, bf16[2560,2560]{1,0:T(8,128)(2,1)} %all-gather.6.cloned.1.call-done.r_ref), custom_call_target="tpu_custom_call" | custom-call | flops 10066329600 | bytes 28835840 | tf_op jit(solution)/shard_map/rotate_hidden/pallas_call | solution.py:207
  317.0 11.3 %mix.2 = (f32[768,1024]{1,0:T(8,128)}, f32[1,1024]{1,0:T(1,128)}) custom-call(s32[1]{0:T(128)} %dynamic_slice.3.len_ref, bf16[768,2560]{1,0:T(8,128)(2,1)} %get-tuple-element.22.act_ref, bf16[32,64,2560]{2,1,0:T(8,128)(2,1)} %bitcast.9), custom_call_target="tpu_custom_call" | custom-call | flops 4026531840 | bytes 13107200 | tf_op jit(solution)/shard_map/mix/pallas_call | solution.py:265
  328.3 9.5 %exchange.4.vrange_ref = f32[1,1024]{1,0:T(1,128)} custom-call(f32[1,1024]{1,0:T(1,128)} %get-tuple-element.25.x_ref), custom_call_target="tpu_custom_call" | custom-call | bytes 30000000 | tf_op jit(solution)/shard_map/exchange/pallas_call | solution.py:84
  337.8 36.9 %update.2 = (f32[768,1]{1,0:T(8,128)}, f32[768,2560]{1,0:T(8,128)}, bf16[768,2560]{1,0:T(8,128)(2,1)}, f32[768,1]{1,0:T(8,128)}, f32[768,1]{1,0:T(8,128)}) custom-call(s32[1]{0:T(128)} %dynamic_slice.3.len_ref, f32[768,1024]{1,0:T(8,128)} %get-tuple-element.24.mixed_ref, f32[1,1024]{1,0:T(1,128)} %exchange.4.vrange_ref, ...), custom_call_target="tpu_custom_call" | custom-call | flops 4026531840 | bytes 28835840 | tf_op jit(solution)/shard_map/update/pallas_call | solution.py:338
  374.7 0.0 copy-start
  374.8 11.4 %mix.3 = (f32[768,1024]{1,0:T(8,128)}, f32[1,1024]{1,0:T(1,128)}) custom-call(s32[1]{0:T(128)} %dynamic_slice.3.len_ref, bf16[768,2560]{1,0:T(8,128)(2,1)} %get-tuple-element.32.act_ref, bf16[32,64,2560]{2,1,0:T(8,128)(2,1)} %bitcast.10), custom_call_target="tpu_custom_call" | custom-call | flops 4026531840 | bytes 13107200 | tf_op jit(solution)/shard_map/mix/pallas_call | solution.py:265
  386.1 12.6 %exchange.6.vrange_ref = f32[1,1024]{1,0:T(1,128)} custom-call(f32[1,1024]{1,0:T(1,128)} %get-tuple-element.34.x_ref), custom_call_target="tpu_custom_call" | custom-call | bytes 30000000 | tf_op jit(solution)/shard_map/exchange/pallas_call | solution.py:84
  398.8 0.0 copy-done
  398.8 0.7 reduce_sum.27
  399.5 0.0 all-gather.10.cloned.1.call-done.o_ref
  399.5 19.8 %update.3 = (f32[768,1]{1,0:T(8,128)}, bf16[768,2560]{1,0:T(8,128)(2,1)}) custom-call(s32[1]{0:T(128)} %dynamic_slice.3.len_ref, f32[768,1024]{1,0:T(8,128)} %get-tuple-element.33.mixed_ref, f32[1,1024]{1,0:T(1,128)} %exchange.6.vrange_ref, bf16[1024,2560]{1,0:T(8,128)(2,1)} %all-gather.10.cloned.1.call-done.o_ref, f32[768,2560]{1,0:T(8,128)} %get-tuple-element.36.resid_ref, ...), custom_call_target="tpu_custom_call" | custom-call | flops 4026531840 | bytes 28835840 | tf_op jit(solution)/shard_map/update/pallas_call | solution.py:338
  419.3 1.7 reduce_sum.28
  422.3 0.5 broadcast_in_dim.4.x_ref
  422.8 10.0 %exchange.7 = f32[1,128]{1,0:T(1,128)} custom-call(f32[1,128]{1,0:T(1,128)} %broadcast_in_dim.4.x_ref), custom_call_target="tpu_custom_call" | custom-call | bytes 30000000 | tf_op jit(solution)/shard_map/exchange/pallas_call | solution.py:84
Async XLA Ops:
  7.2 104.1 %all-gather.6.cloned.1.call-start = ((), (), s32[]{:S(2)}) async-start(), calls=%async_computation | async-start | bytes 13516800 | tf_op jit(solution)/shard_map/all_gather | solution.py:379
  7.9 204.0 %all-gather.12.cloned.1.call-start = ((), (), s32[]{:S(2)}) async-start(), calls=%async_computation.3 | async-start | bytes 10813440 | tf_op jit(solution)/shard_map/all_gather | solution.py:391
  10.8 268.4 %copy-start.1 = (s32[32]{0:T(128)S(1)}, s32[32]{0:T(128)}, u32[]{:S(2)}) copy-start(s32[32]{0:T(128)} %param.11) | copy-start | bytes 388
  120.9 158.3 %all-gather.8.cloned.1.call-start = ((), (), s32[]{:S(2)}) async-start(), calls=%async_computation.1 | async-start | bytes 5406720 | tf_op jit(solution)/shard_map/all_gather | solution.py:396
  211.9 187.6 %all-gather.10.cloned.1.call-start = ((), (), s32[]{:S(2)}) async-start(), calls=%async_computation.2 | async-start | bytes 5406720 | tf_op jit(solution)/shard_map/all_gather | solution.py:396
  374.7 24.0 %copy-start = (f32[768,1]{1,0:T(8,128)S(1)}, f32[768,1]{1,0:T(8,128)}, u32[]{:S(2)}) copy-start(f32[768,1]{1,0:T(8,128)} %get-tuple-element.40) | copy-start | bytes 9220
Sparse Core Ops, SparseCore 0:
  10.8 100.4 all-gather.5
  121.0 90.8 all-gather.11
  215.4 63.8 all-gather.7
  281.9 65.0 all-gather.9
